TPU v7x, 32 devices: a whole 2x2x4 slice. The times are simulated.
32 devices in a mesh: fsdp: 2 (over y), trow: 4 (over x, core), tcol: 4 (over z).
Axes of the slice: x: 2, y: 2, z: 4, core: 2. Of those that a mesh axis runs over, the one named last changes fastest.
Arguments:
- tokens: bfloat16 [512, 4096], P('fsdp', 'tcol'), may hold values from -100 to 100
- w_up: bfloat16 [4096, 16384], P('tcol', ('fsdp', 'trow')), may hold values from -0.1875 to 0.1875
- w_down: bfloat16 [16384, 4096], P(('fsdp', 'trow'), 'tcol'), may hold values from -0.046875 to 0.046875
- cotangent: bfloat16 [512, 4096], P('fsdp', 'tcol'), may hold values from -6 to 6
Outputs:
- mixed: bfloat16 [512, 4096], P('fsdp', 'tcol')
- input_gradient: bfloat16 [512, 4096], P('fsdp', 'tcol')
- grad_up: bfloat16 [4096, 16384], P('tcol', ('fsdp', 'trow'))
- grad_down: bfloat16 [16384, 4096], P(('fsdp', 'trow'), 'tcol')
All inputs are finite; a program needn't handle non-finite values.
Results may differ from a plain program's by a relative error of at most 0.02.
Values may be sent and summed in bfloat16 or wider, within the bound.
No kernel may reach another device: no remote copies, remote signals or barrier semaphores. Data moves between devices by JAX's collectives and lax.ppermute only.
A program may use at most 128 MiB of HBM per device.

v0:
```python
import jax
import jax.numpy as jnp
from jax import lax
from jax.sharding import PartitionSpec as P


def gelu_value(pre):
    phi = 0.5 * (1.0 + jax.scipy.special.erf(pre * 0.7071067811865476))
    return pre * phi


def gelu_slope(pre):
    phi = 0.5 * (1.0 + jax.scipy.special.erf(pre * 0.7071067811865476))
    return phi + pre * jnp.exp(-0.5 * pre * pre) * 0.3989422804014327


def contract(left, right, left_dim, right_dim):
    return lax.dot_general(
        left, right, (((left_dim,), (right_dim,)), ((), ())), preferred_element_type=jnp.float32
    )


def local(tokens, w_up, w_down, cotangent):
    width = tokens.shape[1] * lax.axis_size("tcol")
    input_float = tokens.astype(jnp.float32)
    sum_one, sum_two = lax.psum(
        (jnp.sum(input_float, axis=1), jnp.sum(input_float * input_float, axis=1)), "tcol"
    )
    token_mean = sum_one / width
    var = sum_two / width - token_mean * token_mean
    inverse_stddev = lax.rsqrt(var + 1e-05)
    centered_scaled = (input_float - token_mean[:, None]) * inverse_stddev[:, None]
    normalized_rows = centered_scaled.astype(jnp.bfloat16)
    up_full, down_full = (
        lax.all_gather(w_up, "fsdp", axis=1, tiled=True),
        lax.all_gather(w_down, "fsdp", axis=0, tiled=True),
    )
    pre_full = lax.psum(
        jnp.dot(normalized_rows, up_full, preferred_element_type=jnp.float32).astype(jnp.bfloat16),
        "tcol",
    ).astype(jnp.float32)
    hidden = gelu_value(pre_full).astype(jnp.bfloat16)
    branch = lax.psum(
        jnp.dot(hidden, down_full, preferred_element_type=jnp.float32).astype(jnp.bfloat16), "trow"
    ).astype(jnp.float32)
    mixed = (input_float + branch).astype(jnp.bfloat16)
    down_part = contract(hidden, cotangent, 0, 0)
    grad_down = lax.psum_scatter(
        down_part.astype(jnp.bfloat16), "fsdp", scatter_dimension=0, tiled=True
    )
    dhid = lax.psum(contract(cotangent, down_full, 1, 1).astype(jnp.bfloat16), "tcol").astype(
        jnp.float32
    )
    dpre = (dhid * gelu_slope(pre_full)).astype(jnp.bfloat16)
    up_part = contract(normalized_rows, dpre, 0, 0)
    grad_up = lax.psum_scatter(
        up_part.astype(jnp.bfloat16), "fsdp", scatter_dimension=1, tiled=True
    )
    normed_gradient = lax.psum(contract(dpre, up_full, 1, 1).astype(jnp.bfloat16), "trow").astype(
        jnp.float32
    )
    mean_first, mean_second = lax.psum(
        (jnp.sum(normed_gradient, axis=1), jnp.sum(normed_gradient * centered_scaled, axis=1)),
        "tcol",
    )
    first_moment = mean_first / width
    second_moment = mean_second / width
    input_gradient = cotangent.astype(jnp.float32) + inverse_stddev[:, None] * (
        normed_gradient - first_moment[:, None] - centered_scaled * second_moment[:, None]
    )
    return (mixed, input_gradient.astype(jnp.bfloat16), grad_up, grad_down)


def solution(mesh):
    return jax.shard_map(
        local,
        mesh=mesh,
        in_specs=(
            P("fsdp", "tcol"),
            P("tcol", ("fsdp", "trow")),
            P(("fsdp", "trow"), "tcol"),
            P("fsdp", "tcol"),
        ),
        out_specs=(
            P("fsdp", "tcol"),
            P("fsdp", "tcol"),
            P("tcol", ("fsdp", "trow")),
            P(("fsdp", "trow"), "tcol"),
        ),
        check_vma=False,
    )
```

profile of v0, /device:TPU:0, one launch (start us, length us, event | category | flops | bytes accessed | tf_op | source)
XLA Modules:
  0.0 644.7 jit_solution(2938886579183394449)
XLA Ops:
  7.2 0.7 all-gather.5.cloned.1.call-update
  8.0 0.7 all-gather.3.cloned.1.call-update
  8.7 0.2 convert_reduce_fusion
  9.0 13.5 %all-reduce.1 = (f32[256]{0:T(256)S(1)}, f32[256]{0:T(256)S(1)}) all-reduce(f32[256]{0:T(256)S(1)} %get-tuple-element.7, f32[256]{0:T(256)S(1)} %get-tuple-element.6), channel_id=1, replica_groups=mesh['fsdp'=2,'trow'=4,'tcol'=4] {'tcol'}, use_global_device_ids=true, to_apply=%region_3.0 | all-reduce | flops 512 | bytes 4096 | tf_op jit(solution)/shard_map/psum | solution.py:26
  22.5 93.8 %all-gather.5.cloned.1.call-done = bf16[4096,1024]{1,0:T(8,128)(2,1)} async-done(((bf16[2048,1024]{1,0:T(8,128)(2,1)}), bf16[4096,1024]{1,0:T(8,128)(2,1)}) %all-gather.5.cloned.1.call-update) | async-done | bytes 8388624 | tf_op jit(solution)/shard_map/all_gather | solution.py:36
  116.3 7.1 %convolution_convert_fusion.2 = bf16[256,4096]{1,0:T(8,128)(2,1)} fusion(bf16[256,1024]{1,0:T(8,128)(2,1)S(1)} %copy-done.3, bf16[4096,1024]{1,0:T(8,128)(2,1)} %all-gather.5.cloned.1.call-done), kind=kOutput, calls=%fused_computation.7 | convolution fusion | flops 2148532224 | bytes 11010048 | tf_op jit(solution)/shard_map/dot_general | solution.py:18
  123.3 98.5 %all-gather.3.cloned.1.call-done = bf16[1024,4096]{1,0:T(8,128)(2,1)} async-done(((bf16[1024,2048]{1,0:T(8,128)(2,1)}), bf16[1024,4096]{1,0:T(8,128)(2,1)}) %all-gather.3.cloned.1.call-update) | async-done | bytes 8388624 | tf_op jit(solution)/shard_map/all_gather | solution.py:35
  221.8 7.1 %convolution_convert_fusion.3 = bf16[256,4096]{1,0:T(8,128)(2,1)} fusion(bf16[1024,4096]{1,0:T(8,128)(2,1)} %all-gather.3.cloned.1.call-done, bf16[256,1024]{1,0:T(8,128)(2,1)S(1)} %copy-done, f32[256]{0:T(256)S(1)} %get-tuple-element.19, f32[256]{0:T(256)S(1)} %get-tuple-element.18), kind=kOutput, calls=%fused_computation.8 | convolution fusion | flops 2149580800 | bytes 11012096 | tf_op jit(solution)/shard_map/dot_general | solution.py:39
  229.0 0.0 all-reduce.9.cloned.1.call-start
  229.0 155.1 %all-reduce.7.cloned.1.call-done = (bf16[256,4096]{1,0:T(8,128)(2,1)}, bf16[256,4096]{1,0:T(8,128)(2,1)}) async-done(((bf16[256,4096]{1,0:T(8,128)(2,1)}, bf16[256,4096]{1,0:T(8,128)(2,1)}), (bf16[256,4096]{1,0:T(8,128)(2,1)}, bf16[256,4096]{1,0:T(8,128)(2,1)})) %all-reduce.7.cloned.1.call-update) | async-done | bytes 4194320 | tf_op jit(solution)/shard_map/psum | solution.py:38
  384.2 3.7 fusion.8
  387.9 6.8 %convolution_convert_fusion.5 = bf16[256,1024]{1,0:T(8,128)(2,1)} fusion(bf16[4096,1024]{1,0:T(8,128)(2,1)} %all-gather.5.cloned.1.call-done, bf16[256,4096]{1,0:T(8,128)(2,1)S(1)} %copy-done.1), kind=kOutput, calls=%fused_computation.26 | convolution fusion | flops 2154037248 | bytes 11010048 | tf_op jit(solution)/shard_map/dot_general | solution.py:44
  394.6 3.2 convolution_convert_fusion.4
  397.8 0.2 reduce-scatter.3.cloned.1.call-start
  398.1 5.7 convolution_convert_fusion.1
  403.8 0.0 reduce-scatter.5.cloned.1.call-start
  403.9 1.5 copy-done.2
  405.4 4.7 convolution_convert_fusion
  410.1 23.2 %all-reduce.9.cloned.1.call-done = (bf16[256,1024]{1,0:T(8,128)(2,1)}, bf16[256,1024]{1,0:T(8,128)(2,1)}) async-done(((bf16[256,1024]{1,0:T(8,128)(2,1)}, bf16[256,1024]{1,0:T(8,128)(2,1)}), (bf16[256,1024]{1,0:T(8,128)(2,1)}, bf16[256,1024]{1,0:T(8,128)(2,1)})) %all-reduce.9.cloned.1.call-update) | async-done | bytes 1048592 | tf_op jit(solution)/shard_map/psum | solution.py:43
  433.3 1.5 convert_reduce_fusion.1
  434.7 11.7 %all-reduce = (f32[256]{0:T(256)S(1)}, f32[256]{0:T(256)S(1)}) all-reduce(f32[256]{0:T(256)S(1)} %get-tuple-element.5, f32[256]{0:T(256)S(1)} %get-tuple-element.4), channel_id=1, replica_groups=mesh['fsdp'=2,'trow'=4,'tcol'=4] {'tcol'}, use_global_device_ids=true, to_apply=%region_11.0 | all-reduce | flops 512 | bytes 4096 | tf_op jit(solution)/shard_map/psum | solution.py:62
  446.4 2.6 fusion.12
  449.0 86.8 %reduce-scatter.3.cloned.1.call-done = bf16[1024,2048]{1,0:T(8,128)(2,1)} async-done(((bf16[1024,4096]{1,0:T(8,128)(2,1)}), bf16[1024,2048]{1,0:T(8,128)(2,1)}) %reduce-scatter.3.cloned.1.call-update) | async-done | bytes 4194320 | tf_op jit(solution)/shard_map/reduce_scatter | solution.py:56
  535.8 102.1 %reduce-scatter.5.cloned.1.call-done = bf16[2048,1024]{1,0:T(8,128)(2,1)} async-done(((bf16[4096,1024]{1,0:T(8,128)(2,1)}), bf16[2048,1024]{1,0:T(8,128)(2,1)}) %reduce-scatter.5.cloned.1.call-update) | async-done | bytes 4194320 | tf_op jit(solution)/shard_map/reduce_scatter | solution.py:48
  (21 shorter events, 0.2 us)
Async XLA Ops:
  7.2 1.6 copy-start
  7.2 109.1 %copy-start.3 = (bf16[256,1024]{1,0:T(8,128)(2,1)S(1)}, bf16[256,1024]{1,0:T(8,128)(2,1)}, u32[]{:S(2)}) copy-start(bf16[256,1024]{1,0:T(8,128)(2,1)} %param.7) | copy-start | bytes 1572868
  7.2 109.1 %all-gather.5.cloned.1.call-start = ((), (), s32[]{:S(2)}) async-start(), calls=%async_computation.3 | async-start | bytes 12582912 | tf_op jit(solution)/shard_map/all_gather | solution.py:36
  7.9 213.9 %all-gather.3.cloned.1.call-start = ((), (), s32[]{:S(2)}) async-start(), calls=%async_computation.2 | async-start | bytes 12582912 | tf_op jit(solution)/shard_map/all_gather | solution.py:35
  8.7 375.5 %all-reduce.7.cloned.1.call-start = ((), (), s32[]{:S(2)}) async-start(), calls=%async_computation.6 | async-start | bytes 8388608 | tf_op jit(solution)/shard_map/psum | solution.py:38
  229.0 204.3 %all-reduce.9.cloned.1.call-start = ((), (), s32[]{:S(2)}) async-start(), calls=%async_computation.7 | async-start | bytes 2097152 | tf_op jit(solution)/shard_map/psum | solution.py:43
  384.2 3.7 copy-start.1
  384.2 10.5 %slice-start = ((s8[8388608]{0:T(1024)(128)(4,1)}), s8[4194304]{0:T(1024)(128)(4,1)S(1)}, s32[]{:S(2)}) async-start(s8[8388608]{0:T(1024)(128)(4,1)} %bitcast.8), calls=%async_computation.8 | async-start | bytes 8388608
  387.9 6.8 %slice-start.1 = ((s8[8388608]{0:T(1024)(128)(4,1)}), s8[4194304]{0:T(1024)(128)(4,1)S(1)}, s32[]{:S(2)}) async-start(s8[8388608]{0:T(1024)(128)(4,1)} %bitcast.8), calls=%async_computation.9 | async-start | bytes 8388608
  397.8 138.0 %reduce-scatter.3.cloned.1.call-start = ((), (), s32[]{:S(2)}) async-start(), calls=%async_computation.4 | async-start | bytes 12582912 | tf_op jit(solution)/shard_map/reduce_scatter | solution.py:56
  403.8 1.6 copy-start.2
  403.8 234.1 %reduce-scatter.5.cloned.1.call-start = ((), (), s32[]{:S(2)}) async-start(), calls=%async_computation.5 | async-start | bytes 12582912 | tf_op jit(solution)/shard_map/reduce_scatter | solution.py:48
Sparse Core Ops, SparseCore 0:
  9.5 106.6 all-gather.4
  117.8 103.9 all-gather.2
  229.1 155.0 all-reduce.6
  398.0 35.2 all-reduce.8
  436.0 99.7 reduce-scatter.2
  538.6 99.2 reduce-scatter.4
where the time goes:
time: 645 us
  waiting for transfers between devices  561 us (87%)
  matrix products  34.6 us (5%)
  blocking collectives  25.2 us (4%)
  between operations  14.2 us (2%)
  other arithmetic  7.98 us (1%)
    psum x1, waiting for transfers between devices, local(): lax.psum(jnp.dot(normalized_rows, up_full, preferred_element_type=jnp.flo...  155 us
    reduce_scatter x1, waiting for transfers between devices, local(): lax.psum_scatter(down_part.astype(jnp.bfloat16), 'fsdp', scatter_dimensio...  102 us
    all_gather x1, waiting for transfers between devices, local(): lax.all_gather(w_up, 'fsdp', axis=1, tiled=True)  98.5 us
    all_gather x1, waiting for transfers between devices, local(): lax.all_gather(w_down, 'fsdp', axis=0, tiled=True)  93.8 us
    reduce_scatter x1, waiting for transfers between devices, local(): lax.psum_scatter(up_part.astype(jnp.bfloat16), 'fsdp', scatter_dimension=...  86.8 us
    psum x1, waiting for transfers between devices, local(): lax.psum(jnp.dot(hidden, down_full, preferred_element_type=jnp.float32).a...  23.2 us
    dot_general x4, matrix products, contract(): lax.dot_general(left, right, (((left_dim,), (right_dim,)), ((), ())), pre...  20.7 us
    psum x1, blocking collectives, local(): lax.psum((jnp.sum(input_float, axis=1), jnp.sum(input_float * input_float...  13.5 us
  transfers between devices with their start and end apart: 6, of which 6 were waited for; matrix products, arithmetic and copies ran while one was open for 3% of the time, Pallas kernels for 0%

commit v1 on v0

v1 whole, which is shorter than its diff:
```python
import jax
import jax.numpy as jnp
from jax import lax
from jax.sharding import PartitionSpec as P


def gelu_value(pre):
    phi = 0.5 * (1.0 + jax.scipy.special.erf(pre * 0.7071067811865476))
    return pre * phi


def gelu_slope(pre):
    phi = 0.5 * (1.0 + jax.scipy.special.erf(pre * 0.7071067811865476))
    return phi + pre * jnp.exp(-0.5 * pre * pre) * 0.3989422804014327


def contract(left, right, left_dim, right_dim):
    return lax.dot_general(
        left, right, (((left_dim,), (right_dim,)), ((), ())), preferred_element_type=jnp.float32
    )


def local(tokens, w_up, w_down, cotangent):
    width = tokens.shape[1] * lax.axis_size("tcol")
    input_float = tokens.astype(jnp.float32)
    cot_all = lax.all_gather(cotangent, "fsdp", axis=0, tiled=True)
    sum_one, sum_two = lax.psum(
        (jnp.sum(input_float, axis=1), jnp.sum(input_float * input_float, axis=1)), "tcol"
    )
    token_mean = sum_one / width
    var = sum_two / width - token_mean * token_mean
    inverse_stddev = lax.rsqrt(var + 1e-05)
    centered_scaled = (input_float - token_mean[:, None]) * inverse_stddev[:, None]
    normed = lax.all_gather(centered_scaled.astype(jnp.bfloat16), "fsdp", axis=0, tiled=True)
    dhid = lax.psum(contract(cot_all, w_down, 1, 1).astype(jnp.bfloat16), "tcol").astype(jnp.float32)
    pre = lax.psum(contract(normed, w_up, 1, 0).astype(jnp.bfloat16), "tcol").astype(jnp.float32)
    hidden = gelu_value(pre).astype(jnp.bfloat16)
    dpre = (dhid * gelu_slope(pre)).astype(jnp.bfloat16)
    branch = lax.psum_scatter(
        contract(hidden, w_down, 1, 0).astype(jnp.bfloat16), "fsdp", scatter_dimension=0, tiled=True
    )
    branch = lax.psum(branch, "trow").astype(jnp.float32)
    mixed = (input_float + branch).astype(jnp.bfloat16)
    dnorm = lax.psum_scatter(
        contract(dpre, w_up, 1, 1).astype(jnp.bfloat16), "fsdp", scatter_dimension=0, tiled=True
    )
    dnorm = lax.psum(dnorm, "trow").astype(jnp.float32)
    grad_down = contract(hidden, cot_all, 0, 0).astype(jnp.bfloat16)
    grad_up = contract(normed, dpre, 0, 0).astype(jnp.bfloat16)
    mean_first, mean_second = lax.psum(
        (jnp.sum(dnorm, axis=1), jnp.sum(dnorm * centered_scaled, axis=1)), "tcol"
    )
    first_moment = mean_first / width
    second_moment = mean_second / width
    input_gradient = cotangent.astype(jnp.float32) + inverse_stddev[:, None] * (
        dnorm - first_moment[:, None] - centered_scaled * second_moment[:, None]
    )
    return (mixed, input_gradient.astype(jnp.bfloat16), grad_up, grad_down)


def solution(mesh):
    return jax.shard_map(
        local,
        mesh=mesh,
        in_specs=(
            P("fsdp", "tcol"),
            P("tcol", ("fsdp", "trow")),
            P(("fsdp", "trow"), "tcol"),
            P("fsdp", "tcol"),
        ),
        out_specs=(
            P("fsdp", "tcol"),
            P("fsdp", "tcol"),
            P("tcol", ("fsdp", "trow")),
            P(("fsdp", "trow"), "tcol"),
        ),
        check_vma=False,
    )
```

time: 645 us -> 340 us (0.53)
  waiting for transfers between devices: 561 us -> 255 us
    reduce_scatter x2, waiting for transfers between devices: 189 us -> 30 us  [the longest x1 22.5 us: local(): lax.psum_scatter(contract(hidden, w_down, 1, 0).astype(jnp.bfloat16), 'fs...]
    all_gather x2, waiting for transfers between devices: 192 us -> 35.5 us  [the longest x1 18.8 us: local(): lax.all_gather(centered_scaled.astype(jnp.bfloat16), 'fsdp', axis=0, tile...]
    dot_general x2 -> x0, matrix products: 13.9 us -> none  [the longest x1 7.13 us: local(): jnp.dot(normalized_rows, up_full, preferred_element_type=jnp.float32)]
    dot_general x4 -> x6, matrix products: 20.7 us -> 32.8 us  [contract(): lax.dot_general(left, right, (((left_dim,), (right_dim,)), ((), ())), pre...]
    psum x2, waiting for transfers between devices: 178 us -> 188 us  [the longest x1 155 us: local(): lax.psum(contract(normed, w_up, 1, 0).astype(jnp.bfloat16), 'tcol')]
  transfers between devices with their start and end apart: 6 -> 6, of which waited for: 6 -> 6; matrix products, arithmetic and copies ran while one was open for 3% -> 7% of each run, Pallas kernels for 0% -> 0%
where the time goes in v1:
time: 340 us
  waiting for transfers between devices  255 us (75%)
  matrix products  32.8 us (10%)
  blocking collectives  25.2 us (7%)
  between operations  14.2 us (4%)
  other arithmetic  11.2 us (3%)
    psum x1, waiting for transfers between devices, local(): lax.psum(contract(normed, w_up, 1, 0).astype(jnp.bfloat16), 'tcol')  155 us
    psum x1, waiting for transfers between devices, local(): branch = lax.psum(branch, 'trow').astype(jnp.float32)  33.2 us
    dot_general x6, matrix products, contract(): lax.dot_general(left, right, (((left_dim,), (right_dim,)), ((), ())), pre...  32.8 us
    reduce_scatter x1, waiting for transfers between devices, local(): lax.psum_scatter(contract(hidden, w_down, 1, 0).astype(jnp.bfloat16), 'fs...  22.5 us
    all_gather x1, waiting for transfers between devices, local(): lax.all_gather(centered_scaled.astype(jnp.bfloat16), 'fsdp', axis=0, tile...  18.8 us
    all_gather x1, waiting for transfers between devices, local(): cot_all = lax.all_gather(cotangent, 'fsdp', axis=0, tiled=True)  16.7 us
    psum x1, blocking collectives, local(): lax.psum((jnp.sum(input_float, axis=1), jnp.sum(input_float * input_float...  13.5 us
    psum x1, blocking collectives, local(): lax.psum((jnp.sum(dnorm, axis=1), jnp.sum(dnorm * centered_scaled, axis=1...  11.7 us
  transfers between devices with their start and end apart: 6, of which 6 were waited for; matrix products, arithmetic and copies ran while one was open for 7% of the time, Pallas kernels for 0%

profile of v1, /device:TPU:0, one launch (start us, length us, event | category | flops | bytes accessed | tf_op | source)
XLA Modules:
  0.0 339.8 jit_solution(15268222778512639576)
XLA Ops:
  7.2 1.3 convert_reduce_fusion
  8.5 13.5 %all-reduce.1 = (f32[256]{0:T(256)S(1)}, f32[256]{0:T(256)S(1)}) all-reduce(f32[256]{0:T(256)S(1)} %get-tuple-element.7, f32[256]{0:T(256)S(1)} %get-tuple-element.6), channel_id=1, replica_groups=mesh['fsdp'=2,'trow'=4,'tcol'=4] {'tcol'}, use_global_device_ids=true, to_apply=%region_3.0 | all-reduce | flops 512 | bytes 4096 | tf_op jit(solution)/shard_map/psum | solution.py:27
  22.0 2.1 fusion.16
  24.2 0.7 all-gather.5.cloned.1.call-update
  24.9 18.8 %all-gather.3.cloned.1.call-done = bf16[512,1024]{1,0:T(8,128)(2,1)} async-done(((bf16[256,1024]{1,0:T(8,128)(2,1)}), bf16[512,1024]{1,0:T(8,128)(2,1)}) %all-gather.3.cloned.1.call-update) | async-done | bytes 1048592 | tf_op jit(solution)/shard_map/all_gather | solution.py:34
  43.8 6.2 %convolution_convert_fusion.3 = bf16[512,2048]{1,0:T(8,128)(2,1)} fusion(bf16[512,1024]{1,0:T(8,128)(2,1)} %all-gather.3.cloned.1.call-done, bf16[1024,2048]{1,0:T(8,128)(2,1)} %param.5), kind=kOutput, calls=%fused_computation.17 | convolution fusion | flops 2148532224 | bytes 7340032 | tf_op jit(solution)/shard_map/dot_general | solution.py:18
  49.9 16.7 %all-gather.5.cloned.1.call-done = bf16[512,1024]{1,0:T(8,128)(2,1)} async-done(((bf16[256,1024]{1,0:T(8,128)(2,1)}), bf16[512,1024]{1,0:T(8,128)(2,1)}) %all-gather.5.cloned.1.call-update) | async-done | bytes 1048592 | tf_op jit(solution)/shard_map/all_gather | solution.py:26
  66.6 6.2 %convolution_convert_fusion.2 = bf16[512,2048]{1,0:T(8,128)(2,1)} fusion(bf16[512,1024]{1,0:T(8,128)(2,1)} %all-gather.5.cloned.1.call-done, bf16[2048,1024]{1,0:T(8,128)(2,1)} %param.6), kind=kOutput, calls=%fused_computation.16 | convolution fusion | flops 2148532224 | bytes 7340032 | tf_op jit(solution)/shard_map/dot_general | solution.py:18
  72.8 0.0 reduce-scatter.5.cloned.1.call-start
  72.9 155.1 %all-reduce.7.cloned.1.call-done = (bf16[512,2048]{1,0:T(8,128)(2,1)}, bf16[512,2048]{1,0:T(8,128)(2,1)}) async-done(((bf16[512,2048]{1,0:T(8,128)(2,1)}, bf16[512,2048]{1,0:T(8,128)(2,1)}), (bf16[512,2048]{1,0:T(8,128)(2,1)}, bf16[512,2048]{1,0:T(8,128)(2,1)})) %all-reduce.7.cloned.1.call-update) | async-done | bytes 4194320 | tf_op jit(solution)/shard_map/psum | solution.py:36
  228.0 3.7 %fusion.8 = bf16[512,2048]{1,0:T(8,128)(2,1)S(1)} fusion(bf16[512,2048]{1,0:T(8,128)(2,1)} %get-tuple-element.12, bf16[512,2048]{1,0:T(8,128)(2,1)} %get-tuple-element.13), kind=kLoop, calls=%fused_computation.13 | loop fusion | flops 12582912 | bytes 6291456 | tf_op jit(solution)/shard_map/convert_element_type | solution.py:38
  231.7 1.3 copy-done.2
  233.0 3.4 convolution_convert_fusion.4
  236.4 0.0 reduce-scatter.3.cloned.1.call-start
  236.5 5.7 %convolution_convert_fusion.5 = bf16[512,1024]{1,0:T(8,128)(2,1)} fusion(bf16[2048,1024]{1,0:T(8,128)(2,1)} %param.6, bf16[512,2048]{1,0:T(8,128)(2,1)S(1)} %copy-done.1), kind=kOutput, calls=%fused_computation.26 | convolution fusion | flops 2154299392 | bytes 7340032 | tf_op jit(solution)/shard_map/dot_general | solution.py:18
  242.2 0.2 all-reduce.9.cloned.1.call-start
  242.5 6.0 %convolution_convert_fusion.1 = bf16[1024,2048]{1,0:T(8,128)(2,1)} fusion(bf16[512,1024]{1,0:T(8,128)(2,1)S(1)} %copy-done.5, bf16[512,2048]{1,0:T(8,128)(2,1)} %copy-done.2), kind=kOutput, calls=%fused_computation.15 | convolution fusion | flops 2149580800 | bytes 7340032 | tf_op jit(solution)/shard_map/dot_general | solution.py:18
  248.5 7.5 %reduce-scatter.5.cloned.1.call-done = bf16[256,1024]{1,0:T(8,128)(2,1)} async-done(((bf16[512,1024]{1,0:T(8,128)(2,1)}), bf16[256,1024]{1,0:T(8,128)(2,1)}) %reduce-scatter.5.cloned.1.call-update) | async-done | bytes 524304 | tf_op jit(solution)/shard_map/reduce_scatter | solution.py:44
  256.0 22.5 %reduce-scatter.3.cloned.1.call-done = bf16[256,1024]{1,0:T(8,128)(2,1)} async-done(((bf16[512,1024]{1,0:T(8,128)(2,1)}), bf16[256,1024]{1,0:T(8,128)(2,1)}) %reduce-scatter.3.cloned.1.call-update) | async-done | bytes 524304 | tf_op jit(solution)/shard_map/reduce_scatter | solution.py:39
  278.5 5.4 %convolution_convert_fusion = bf16[2048,1024]{1,0:T(8,128)(2,1)} fusion(bf16[512,1024]{1,0:T(8,128)(2,1)} %all-gather.5.cloned.1.call-done, bf16[512,2048]{1,0:T(8,128)(2,1)S(1)} %copy-done.1), kind=kOutput, calls=%fused_computation.14 | convolution fusion | flops 2155872256 | bytes 7340032 | tf_op jit(solution)/shard_map/dot_general | solution.py:18
  283.9 33.2 %all-reduce.9.cloned.1.call-done = (bf16[256,1024]{1,0:T(8,128)(2,1)}, bf16[256,1024]{1,0:T(8,128)(2,1)}) async-done(((bf16[256,1024]{1,0:T(8,128)(2,1)}, bf16[256,1024]{1,0:T(8,128)(2,1)}), (bf16[256,1024]{1,0:T(8,128)(2,1)}, bf16[256,1024]{1,0:T(8,128)(2,1)})) %all-reduce.9.cloned.1.call-update) | async-done | bytes 1048592 | tf_op jit(solution)/shard_map/psum | solution.py:42
  317.1 1.5 convert_reduce_fusion.1
  318.6 11.7 %all-reduce = (f32[256]{0:T(256)S(1)}, f32[256]{0:T(256)S(1)}) all-reduce(f32[256]{0:T(256)S(1)} %get-tuple-element.5, f32[256]{0:T(256)S(1)} %get-tuple-element.4), channel_id=1, replica_groups=mesh['fsdp'=2,'trow'=4,'tcol'=4] {'tcol'}, use_global_device_ids=true, to_apply=%region_13.0 | all-reduce | flops 512 | bytes 4096 | tf_op jit(solution)/shard_map/psum | solution.py:50
  330.3 2.6 fusion.12
  (21 shorter events, 0.2 us)
Async XLA Ops:
  7.2 36.6 %all-gather.3.cloned.1.call-start = ((), (), s32[]{:S(2)}) async-start(), calls=%async_computation.2 | async-start | bytes 1572864 | tf_op jit(solution)/shard_map/all_gather | solution.py:34
  24.1 42.5 %all-gather.5.cloned.1.call-start = ((), (), s32[]{:S(2)}) async-start(), calls=%async_computation.4 | async-start | bytes 1572864 | tf_op jit(solution)/shard_map/all_gather | solution.py:26
  24.9 203.1 %all-reduce.7.cloned.1.call-start = ((), (), s32[]{:S(2)}) async-start(), calls=%async_computation.6 | async-start | bytes 8388608 | tf_op jit(solution)/shard_map/psum | solution.py:36
  72.8 183.1 %reduce-scatter.5.cloned.1.call-start = ((), (), s32[]{:S(2)}) async-start(), calls=%async_computation.5 | async-start | bytes 1572864 | tf_op jit(solution)/shard_map/reduce_scatter | solution.py:44
  228.0 5.0 %copy-start.4 = (bf16[1024,2048]{1,0:T(8,128)(2,1)S(1)}, bf16[1024,2048]{1,0:T(8,128)(2,1)}, u32[]{:S(2)}) copy-start(bf16[1024,2048]{1,0:T(8,128)(2,1)} %param.5) | copy-start | bytes 12582916
  231.7 1.3 copy-start.2
  233.0 3.4 %copy-start.1 = (bf16[512,2048]{1,0:T(8,128)(2,1)S(1)}, bf16[512,2048]{1,0:T(8,128)(2,1)}, u32[]{:S(2)}) copy-start(bf16[512,2048]{1,0:T(8,128)(2,1)} %get-tuple-element.12) | copy-start | bytes 6291460
  236.4 6.1 %copy-start.5 = (bf16[512,1024]{1,0:T(8,128)(2,1)S(1)}, bf16[512,1024]{1,0:T(8,128)(2,1)}, u32[]{:S(2)}) copy-start(bf16[512,1024]{1,0:T(8,128)(2,1)} %all-gather.3.cloned.1.call-done) | copy-start | bytes 3145732
  236.4 42.0 %reduce-scatter.3.cloned.1.call-start = ((), (), s32[]{:S(2)}) async-start(), calls=%async_computation.3 | async-start | bytes 1572864 | tf_op jit(solution)/shard_map/reduce_scatter | solution.py:39
  242.2 74.9 %all-reduce.9.cloned.1.call-start = ((), (), s32[]{:S(2)}) async-start(), calls=%async_computation.7 | async-start | bytes 2097152 | tf_op jit(solution)/shard_map/psum | solution.py:42
  278.5 38.6 %copy-start = (bf16[256,1024]{1,0:T(8,128)(2,1)S(1)}, bf16[256,1024]{1,0:T(8,128)(2,1)}, u32[]{:S(2)}) copy-start(bf16[256,1024]{1,0:T(8,128)(2,1)} %param.4) | copy-start | bytes 1572868
  278.5 51.8 %copy-start.3 = (bf16[256,1024]{1,0:T(8,128)(2,1)S(1)}, bf16[256,1024]{1,0:T(8,128)(2,1)}, u32[]{:S(2)}) copy-start(bf16[256,1024]{1,0:T(8,128)(2,1)} %param.7) | copy-start | bytes 1572868
Sparse Core Ops, SparseCore 0:
  24.2 19.4 all-gather.2
  45.3 21.2 all-gather.4
  73.0 155.0 all-reduce.6
  236.5 19.3 reduce-scatter.4
  258.0 20.3 reduce-scatter.2
  280.8 36.3 all-reduce.8
